TPU v7x, 32 devices: a whole 2x2x4 slice. The times are simulated.
32 devices in a mesh: mem: 2 (over x), col: 16 (over z, y, core).
Axes of the slice: x: 2, y: 2, z: 4, core: 2. Of those that a mesh axis runs over, the one named last changes fastest.
Arguments:
- state_a: bfloat16 [64, 1048576], P('mem', 'col'), may hold values from -12 to 12
- state_b: bfloat16 [64, 1048576], P('mem', 'col'), may hold values from -12 to 12
- obs_index: int32 [2, 8192, 16], P(None, ('col', 'mem')), may hold values from 0 to 127
- observation_count: int32 [2, 8192], P(None, ('col', 'mem')), may hold values from 1 to 16, as said below
- obs_value: float32 [2, 8192, 16], P(None, ('col', 'mem')), may hold values from -32 to 32
- obs_weight: float32 [2, 8192, 16], P(None, ('col', 'mem')), may hold values from 0.02 to 0.2
Outputs:
- analysis_a: bfloat16 [64, 1048576], P(None, ('col', 'mem'))
- analysis_b: bfloat16 [64, 1048576], P(None, ('col', 'mem'))
- transform: float32 [64, 64], replicated
Inputs may be any that keep to these rules, and one draw needn't show every extreme that they name: Slot s of block b of group g is an observation when s < observation_count[g, b]; for each group, every aligned run of 256 blocks holds a block with all 16 slots live.
All inputs are finite; a program needn't handle non-finite values.
Results may differ from a plain program's by a relative error of at most 0.005.
Values may be sent and summed in bfloat16 or wider, within the bound.
A program may use at most 64 MiB of HBM per device.

v0:
```python
import jax
import jax.numpy as jnp
from jax import lax
from jax.sharding import PartitionSpec as P

ITERS = 24


def inverse_root(amat):
    scale = jnp.sqrt(jnp.sum(amat * amat))
    eye = jnp.eye(amat.shape[0], dtype=jnp.float32)

    def forward_step(step, carry):
        yn, zn = carry
        tm = 1.5 * eye - 0.5 * jnp.dot(zn, yn, precision=lax.Precision.HIGHEST)
        return (
            jnp.dot(yn, tm, precision=lax.Precision.HIGHEST),
            jnp.dot(tm, zn, precision=lax.Precision.HIGHEST),
        )

    yn, zn = lax.fori_loop(0, ITERS, forward_step, (amat / scale, eye))
    return (zn, scale)


def make_transform(gram_product, cross, misfit, total):
    members = gram_product.shape[0]
    scl = (members - 1.0) / total
    gs = scl * gram_product
    bs = scl * cross
    qval = scl * misfit
    tval = jnp.trace(gs)
    rho = (1.0 + qval / (members - 1.0)) / (1.0 + tval / (members - 1.0))
    amat = (members - 1.0) / rho * jnp.eye(members, dtype=jnp.float32) + gs
    zn, scale = inverse_root(amat)
    pmat = jnp.dot(zn, zn, precision=lax.Precision.HIGHEST) / scale
    wbar = jnp.dot(pmat, bs, precision=lax.Precision.HIGHEST)
    return jnp.sqrt(members - 1.0) * zn / jnp.sqrt(scale) + wbar[:, None]


def shards(state_a, state_b, obs_index, observation_count, obs_value, obs_weight):
    members = state_a.shape[0]
    group_column_sets = state_a.shape[1]
    nmem = lax.axis_size("mem")
    piece = group_column_sets // nmem
    everyone = members * nmem
    nblk = obs_index.shape[1]
    slots = obs_index.shape[2]
    width = nblk * slots
    live = (
        lax.broadcasted_iota(jnp.int32, (2, nblk, slots), 2) < observation_count[:, :, None]
    ).astype(jnp.float32)
    live = live.reshape(2, width)
    weights = live * obs_weight.reshape(2, width)
    observed = obs_value.reshape(2, width)

    def observe(columns, index, blocks):
        lanes = lax.broadcasted_iota(jnp.int32, (blocks, slots, 128), 2)
        onehot = (index[:, :, None] == lanes).astype(jnp.bfloat16)
        taken = jnp.einsum(
            "kbc,bsc->kbs",
            columns.reshape(columns.shape[0], blocks, 128),
            onehot,
            preferred_element_type=jnp.float32,
        )
        return taken.reshape(columns.shape[0], blocks * slots)

    def statistics(hx, group):
        hmean = jnp.mean(hx, axis=0)
        anomaly_rows = hx - hmean[None]
        innov = observed[group] - hmean
        wt = weights[group]
        scaled_anomaly = anomaly_rows * wt[None]
        gram_product = jnp.einsum(
            "kn,ln->kl", scaled_anomaly, anomaly_rows, precision=lax.Precision.HIGHEST
        )
        cross = jnp.einsum("kn,n->k", scaled_anomaly, innov, precision=lax.Precision.HIGHEST)
        misfit = jnp.sum(wt * innov * innov)
        extra = jnp.stack([misfit, jnp.sum(live[group])])
        return (gram_product, cross, extra)

    def regroup(state):
        return state.reshape(members, nmem, piece)

    all_index = lax.all_gather(obs_index, "mem", axis=1, tiled=True)
    local_hx = jnp.stack(
        [observe(state_a, all_index[0], nmem * nblk), observe(state_b, all_index[1], nmem * nblk)]
    ).astype(jnp.bfloat16)
    moved_hx = lax.all_to_all(
        local_hx.reshape(2, members, nmem, width), "mem", split_axis=2, concat_axis=1, tiled=True
    )
    hx_all = moved_hx.reshape(2, everyone, width).astype(jnp.float32)
    first = statistics(hx_all[0], 0)
    second = statistics(hx_all[1], 1)
    gram_product, cross, extra = lax.psum(
        (first[0] + second[0], first[1] + second[1], first[2] + second[2]), ("mem", "col")
    )
    moved_a, moved_b = (
        lax.all_to_all(regroup(state_a), "mem", split_axis=1, concat_axis=0, tiled=True),
        lax.all_to_all(regroup(state_b), "mem", split_axis=1, concat_axis=0, tiled=True),
    )
    columns = [moved_a.reshape(everyone, piece), moved_b.reshape(everyone, piece)]
    misfit = extra[0]
    total = extra[1]
    transform = make_transform(gram_product, cross, misfit, total)
    wb = transform.astype(jnp.bfloat16)
    column_total = jnp.sum(wb.astype(jnp.float32), axis=0)
    ones = jnp.ones((everyone,), jnp.bfloat16)

    def analyse(cols):
        xmean = jnp.dot(ones, cols, preferred_element_type=jnp.float32) / everyone
        mixed = jnp.dot(wb.T, cols, preferred_element_type=jnp.float32)
        return (mixed + xmean[None, :] * (1.0 - column_total)[:, None]).astype(jnp.bfloat16)

    return (analyse(columns[0]), analyse(columns[1]), transform)


def solution(mesh):
    return jax.shard_map(
        shards,
        mesh=mesh,
        in_specs=(
            P("mem", "col"),
            P("mem", "col"),
            P(None, ("col", "mem"), None),
            P(None, ("col", "mem")),
            P(None, ("col", "mem"), None),
            P(None, ("col", "mem"), None),
        ),
        out_specs=(P(None, ("col", "mem")), P(None, ("col", "mem")), P()),
        check_vma=False,
    )
```

profile of v0, /device:TPU:0, one launch (start us, length us, event | category | flops | bytes accessed | tf_op | source)
XLA Modules:
  0.0 192.1 jit_solution(10022677384199641888)
XLA Ops:
  0.6 5.8 %all_gather.3 = s32[2,512,16]{1,2,0:T(8,128)S(1)} all-gather(s32[2,256,16]{1,2,0:T(8,128)} %param.10), channel_id=1, replica_groups=mesh['mem'=2,'col'=16] {'mem'}, dimensions={1}, use_global_device_ids=true | all-gather | bytes 98304 | tf_op jit(solution)/shard_map/all_gather | solution.py:84
  6.7 4.6 %fusion.16 = bf16[512,16,32]{2,1,0:T(8,128)(2,1)S(1)} fusion(s32[512,16]{1,0:T(8,128)S(1)} %copy.40, bf16[32,65536]{1,0:T(8,128)(2,1)} %param.9), kind=kOutput, calls=%fused_computation.23 | convolution fusion | flops 68419584 | bytes 4751360 | tf_op jit(solution)/shard_map/kbc,bsc->kbs/dot_general | solution.py:59
  11.3 0.8 copy.43
  12.1 4.6 %fusion.13 = bf16[512,16,32]{2,1,0:T(8,128)(2,1)S(1)} fusion(s32[512,16]{1,0:T(8,128)S(1)} %copy.38, bf16[32,65536]{1,0:T(8,128)(2,1)} %param.8), kind=kOutput, calls=%fused_computation.22 | convolution fusion | flops 68419584 | bytes 4751360 | tf_op jit(solution)/shard_map/kbc,bsc->kbs/dot_general | solution.py:59
  16.7 0.8 copy.42
  17.5 1.1 pad_maximum_fusion
  18.6 3.6 %all-to-all-start = ((bf16[2,32,2,4096]{3,1,0,2:T(8,128)(2,1)}), bf16[2,32,2,4096]{3,1,0,2:T(8,128)(2,1)S(1)}, u32[]{:S(2)}, u32[]{:S(2)}) async-start(bf16[2,32,2,4096]{3,1,0,2:T(8,128)(2,1)} %pad_maximum_fusion), calls=%async_computation | async-start | bytes 2097152 | tf_op jit(solution)/shard_map/all_to_all | solution.py:88
  23.2 0.7 slice_reduce_fusion
  24.2 4.6 %copy.70 = bf16[4,2,8,32768]{3,2,0,1:T(8,128)(2,1)} copy(bf16[4,2,8,32768]{3,2,1,0:T(8,128)(2,1)} %bitcast.125) | data formatting | bytes 8388608 | tf_op jit(solution)/shard_map/reshape | solution.py:82
  28.8 2.3 %copy.71 = bf16[4,2,8,32768]{3,2,0,1:T(8,128)(2,1)} copy(bf16[4,2,8,32768]{3,2,1,0:T(8,128)(2,1)S(1)} %bitcast.126) | data formatting | bytes 8388608 | tf_op jit(solution)/shard_map/reshape | solution.py:82
  31.2 4.0 %all-to-all-done = bf16[2,32,2,4096]{3,1,0,2:T(8,128)(2,1)S(1)} async-done(((bf16[2,32,2,4096]{3,1,0,2:T(8,128)(2,1)}), bf16[2,32,2,4096]{3,1,0,2:T(8,128)(2,1)S(1)}, u32[]{:S(2)}, u32[]{:S(2)}) %all-to-all-start) | async-done | bytes 1048608 | tf_op jit(solution)/shard_map/all_to_all | solution.py:88
  35.1 5.6 %all-to-all-start.2 = ((bf16[32,2,32768]{2,0,1:T(8,128)(2,1)}), bf16[32,2,32768]{2,0,1:T(8,128)(2,1)}, u32[]{:S(2)}, u32[]{:S(2)}) async-start(bf16[32,2,32768]{2,0,1:T(8,128)(2,1)} %bitcast.124), calls=%async_computation.2 | async-start | bytes 8388608 | tf_op jit(solution)/shard_map/all_to_all | solution.py:99
  41.0 0.3 slice_reduce_fusion.2
  41.3 0.6 fusion.38
  42.1 0.7 fusion.39
  43.0 2.6 %maximum_add_fusion = f32[2]{0:T(128)S(1)} fusion(f32[1]{0:T(128)} %bitcast.10, f32[1]{0:T(128)} %bitcast.9, f32[1]{0:T(128)} %bitcast.14, f32[1]{0:T(128)} %bitcast.13), kind=kLoop, calls=%fused_computation.71 | loop fusion | flops 6 | bytes 24 | tf_op jit(solution)/shard_map/add | solution.py:95
  45.8 0.9 convolution_bitcast_fusion.1
  46.7 1.0 fusion.19
  47.7 1.0 fusion.25
  48.7 1.0 convolution_add_fusion.2
  49.7 71.5 %all-reduce = (f32[64,64]{1,0:T(8,128)S(1)}, f32[2]{0:T(128)S(1)}, f32[64]{0:T(128)S(1)}) all-reduce(f32[64,64]{1,0:T(8,128)S(1)} %convolution_add_fusion.2, f32[2]{0:T(128)S(1)} %maximum_add_fusion, f32[64]{0:T(128)S(1)} %fusion.19), channel_id=1, replica_groups=mesh['mem'=2,'col'=16] {'mem','col'}, use_global_device_ids=true, to_apply=%region_7.0 | all-reduce | flops 4162 | bytes 33296 | tf_op jit(solution)/shard_map/psum | solution.py:94
  121.2 0.6 fusion.53
  123.1 0.6 select_reduce_fusion
  124.4 0.6 multiply_reduce_fusion
  125.8 5.8 %all-to-all-start.1 = ((bf16[32,2,32768]{2,0,1:T(8,128)(2,1)}), bf16[32,2,32768]{2,0,1:T(8,128)(2,1)}, u32[]{:S(2)}, u32[]{:S(2)}) async-start(bf16[32,2,32768]{2,0,1:T(8,128)(2,1)} %bitcast.123), calls=%async_computation.1 | async-start | bytes 8388608 | tf_op jit(solution)/shard_map/all_to_all | solution.py:98
  131.6 15.5 %while.13 = (s32[]{:T(128)}, f32[64,64]{0,1:T(8,128)S(1)}, f32[64,64]{1,0:T(8,128)S(1)}, s32[]{:T(128)}) while((s32[]{:T(128)}, f32[64,64]{0,1:T(8,128)S(1)}, f32[64,64]{1,0:T(8,128)S(1)}, s32[]{:T(128)}) %tuple.41), condition=%wide.region_11.12_spmd.clone, body=%wide.region_10.11_spmd.clone.sunk | while | flops 9453570 | bytes 213045 | solution.py:21
  132.6 0.2 convolution_bitcast_fusion.5
  147.5 2.8 %fusion.42 = f32[1,32768]{1,0:T(1,128)S(1)} fusion(bf16[64,32768]{1,0:T(8,128)(2,1)} %bitcast.35), kind=kOutput, calls=%fused_computation.74 | convolution fusion | flops 4194304 | bytes 4325376 | tf_op jit(solution)/shard_map/dot_general | solution.py:110
  150.4 27.9 %all-to-all-done.1 = bf16[32,2,32768]{2,0,1:T(8,128)(2,1)} async-done(((bf16[32,2,32768]{2,0,1:T(8,128)(2,1)}), bf16[32,2,32768]{2,0,1:T(8,128)(2,1)}, u32[]{:S(2)}, u32[]{:S(2)}) %all-to-all-start.1) | async-done | bytes 4194336 | tf_op jit(solution)/shard_map/all_to_all | solution.py:98
  178.3 2.8 %fusion.44 = f32[1,32768]{1,0:T(1,128)S(1)} fusion(bf16[64,32768]{1,0:T(8,128)(2,1)} %bitcast.29), kind=kOutput, calls=%fused_computation.76 | convolution fusion | flops 4194304 | bytes 4325376 | tf_op jit(solution)/shard_map/dot_general | solution.py:110
  181.1 5.5 %fusion.4 = bf16[64,32768]{1,0:T(8,128)(2,1)} fusion(bf16[64,32768]{1,0:T(8,128)(2,1)} %bitcast.35, f32[32768]{0:T(1024)S(1)} %broadcast_multiply_fusion, f32[64]{0:T(128)S(1)} %broadcast_subtract_fusion, f32[64,64]{1,0:T(8,128)S(1)} %get-tuple-element.60), kind=kOutput, calls=%fused_computation.8 | convolution fusion | flops 274731008 | bytes 8536320 | tf_op jit(solution)/shard_map/dot_general | solution.py:111
  186.6 5.5 %fusion.3 = bf16[64,32768]{1,0:T(8,128)(2,1)} fusion(bf16[64,32768]{1,0:T(8,128)(2,1)} %bitcast.29, f32[64]{0:T(128)S(1)} %broadcast_subtract_fusion, f32[32768]{0:T(1024)S(1)} %broadcast_multiply_fusion.1, f32[64,64]{1,0:T(8,128)S(1)} %get-tuple-element.60), kind=kOutput, calls=%fused_computation.7 | convolution fusion | flops 274731008 | bytes 8536320 | tf_op jit(solution)/shard_map/dot_general | solution.py:111
  (164 shorter events, 16.9 us)
Async XLA Ops:
  16.6 5.5 %copy-start.3 = (f32[2,256,16]{1,2,0:T(8,128)S(1)}, f32[2,256,16]{1,2,0:T(8,128)}, u32[]{:S(2)}) copy-start(f32[2,256,16]{1,2,0:T(8,128)} %param.12) | copy-start | bytes 98308
  16.7 6.1 %copy-start.2 = (f32[2,256,16]{1,2,0:T(8,128)S(1)}, f32[2,256,16]{1,2,0:T(8,128)}, u32[]{:S(2)}) copy-start(f32[2,256,16]{1,2,0:T(8,128)} %param.13) | copy-start | bytes 98308
  16.7 6.4 %copy-start.4 = (s32[2,256]{1,0:T(2,128)S(1)}, s32[2,256]{1,0:T(2,128)}, u32[]{:S(2)}) copy-start(s32[2,256]{1,0:T(2,128)} %param.11) | copy-start | bytes 6148
  18.6 16.6 %all-to-all-start = ((bf16[2,32,2,4096]{3,1,0,2:T(8,128)(2,1)}), bf16[2,32,2,4096]{3,1,0,2:T(8,128)(2,1)S(1)}, u32[]{:S(2)}, u32[]{:S(2)}) async-start(bf16[2,32,2,4096]{3,1,0,2:T(8,128)(2,1)} %pad_maximum_fusion), calls=%async_computation | async-start | bytes 2097152 | tf_op jit(solution)/shard_map/all_to_all | solution.py:88
  24.1 4.6 %copy-start = (bf16[32,65536]{1,0:T(8,128)(2,1)S(1)}, bf16[32,65536]{1,0:T(8,128)(2,1)}, u32[]{:S(2)}) copy-start(bf16[32,65536]{1,0:T(8,128)(2,1)} %param.8) | copy-start | bytes 12582916
  35.1 90.6 %all-to-all-start.2 = ((bf16[32,2,32768]{2,0,1:T(8,128)(2,1)}), bf16[32,2,32768]{2,0,1:T(8,128)(2,1)}, u32[]{:S(2)}, u32[]{:S(2)}) async-start(bf16[32,2,32768]{2,0,1:T(8,128)(2,1)} %bitcast.124), calls=%async_computation.2 | async-start | bytes 8388608 | tf_op jit(solution)/shard_map/all_to_all | solution.py:99
  125.8 52.5 %all-to-all-start.1 = ((bf16[32,2,32768]{2,0,1:T(8,128)(2,1)}), bf16[32,2,32768]{2,0,1:T(8,128)(2,1)}, u32[]{:S(2)}, u32[]{:S(2)}) async-start(bf16[32,2,32768]{2,0,1:T(8,128)(2,1)} %bitcast.123), calls=%async_computation.1 | async-start | bytes 8388608 | tf_op jit(solution)/shard_map/all_to_all | solution.py:98
  147.5 39.1 %copy-start.1 = (f32[64,64]{1,0:T(8,128)}, f32[64,64]{1,0:T(8,128)S(1)}, u32[]{:S(2)}) copy-start(f32[64,64]{1,0:T(8,128)S(1)} %get-tuple-element.60) | copy-start | bytes 49156
where the time goes:
time: 193 us; the launch traced here: 192 us
  blocking collectives  77.2 us (40%)
  matrix products  44 us (23%)
  waiting for transfers between devices  31.8 us (16%)
  starting transfers between devices  15 us (8%)
  local copies, waits for them, and re-layouts  11.2 us (6%)
  other arithmetic  7.89 us (4%)
  between operations  3.67 us (2%)
    psum x1, blocking collectives, shards(): lax.psum((first[0] + second[0], first[1] + second[1], first[2] + second[2...  71.5 us
    all_to_all x1, waiting for transfers between devices, shards(): lax.all_to_all(regroup(state_a), 'mem', split_axis=1, concat_axis=0, tile...  27.9 us
    dot_general x2, matrix products, analyse(): mixed = jnp.dot(wb.T, cols, preferred_element_type=jnp.float32)  11 us
    dot_general x2, matrix products, observe(): jnp.einsum('kbc,bsc->kbs', columns.reshape(columns.shape[0], blocks, 128)...  9.13 us
    reshape x2, local copies, waits for them, and re-layouts, regroup(): return state.reshape(members, nmem, piece)  6.94 us
    all_gather x1, blocking collectives, shards(): all_index = lax.all_gather(obs_index, 'mem', axis=1, tiled=True)  5.79 us
    all_to_all x1, starting transfers between devices, shards(): lax.all_to_all(regroup(state_a), 'mem', split_axis=1, concat_axis=0, tile...  5.79 us
    dot_general x2, matrix products, analyse(): xmean = jnp.dot(ones, cols, preferred_element_type=jnp.float32) / everyone  5.68 us
  transfers between devices with their start and end apart: 3, of which 2 were waited for; matrix products, arithmetic and copies ran while one was open for 19% of the time, Pallas kernels for 0%

commit v1 on v0

--- a/solution.py
+++ b/solution.py
@@ -4,6 +4,11 @@
 from jax.sharding import PartitionSpec as P
 
 ITERS = 24
+
+
+def one_after_other(value, inner_axis, outer_axis):
+    inner = lax.psum(value, inner_axis)
+    return lax.psum(inner, outer_axis)
 
 
 def inverse_root(amat):
@@ -91,8 +96,8 @@
     hx_all = moved_hx.reshape(2, everyone, width).astype(jnp.float32)
     first = statistics(hx_all[0], 0)
     second = statistics(hx_all[1], 1)
-    gram_product, cross, extra = lax.psum(
-        (first[0] + second[0], first[1] + second[1], first[2] + second[2]), ("mem", "col")
+    gram_product, cross, extra = one_after_other(
+        (first[0] + second[0], first[1] + second[1], first[2] + second[2]), "mem", "col"
     )
     moved_a, moved_b = (
         lax.all_to_all(regroup(state_a), "mem", split_axis=1, concat_axis=0, tiled=True),

time: 193 us -> 216 us (1.12)
  blocking collectives: 77.2 us -> 104 us
  waiting for transfers between devices: 31.8 us -> 28.3 us
    psum x1 -> x2, blocking collectives: 71.5 us -> 98 us  [the longest x1 58.6 us: one_after_other(): return lax.psum(inner, outer_axis)]
    all_to_all x1, waiting for transfers between devices: 27.9 us -> 24.3 us  [shards(): lax.all_to_all(regroup(state_a), 'mem', split_axis=1, concat_axis=0, tile...]
  transfers between devices with their start and end apart: 3 -> 3, of which waited for: 2 -> 2; matrix products, arithmetic and copies ran while one was open for 19% -> 17% of each run, Pallas kernels for 0% -> 0%
where the time goes in v1:
time: 216 us; the launch traced here: 215 us
  blocking collectives  104 us (48%)
  matrix products  44 us (20%)
  waiting for transfers between devices  28.3 us (13%)
  starting transfers between devices  15 us (7%)
  local copies, waits for them, and re-layouts  11.2 us (5%)
  other arithmetic  7.9 us (4%)
  between operations  3.67 us (2%)
    psum x1, blocking collectives, one_after_other(): return lax.psum(inner, outer_axis)  58.6 us
    psum x1, blocking collectives, one_after_other(): inner = lax.psum(value, inner_axis)  39.4 us
    all_to_all x1, waiting for transfers between devices, shards(): lax.all_to_all(regroup(state_a), 'mem', split_axis=1, concat_axis=0, tile...  24.3 us
    dot_general x2, matrix products, analyse(): mixed = jnp.dot(wb.T, cols, preferred_element_type=jnp.float32)  11 us
    dot_general x2, matrix products, observe(): jnp.einsum('kbc,bsc->kbs', columns.reshape(columns.shape[0], blocks, 128)...  9.13 us
    reshape x2, local copies, waits for them, and re-layouts, regroup(): return state.reshape(members, nmem, piece)  6.94 us
    all_gather x1, blocking collectives, shards(): all_index = lax.all_gather(obs_index, 'mem', axis=1, tiled=True)  5.79 us
    all_to_all x1, starting transfers between devices, shards(): lax.all_to_all(regroup(state_a), 'mem', split_axis=1, concat_axis=0, tile...  5.79 us
  transfers between devices with their start and end apart: 3, of which 2 were waited for; matrix products, arithmetic and copies ran while one was open for 17% of the time, Pallas kernels for 0%

profile of v1, /device:TPU:0, one launch (start us, length us, event | category | flops | bytes accessed | tf_op | source)
XLA Modules:
  0.0 215.1 jit_solution(15622349304442020659)
XLA Ops:
  0.6 5.8 %all_gather.3 = s32[2,512,16]{1,2,0:T(8,128)S(1)} all-gather(s32[2,256,16]{1,2,0:T(8,128)} %param.10), channel_id=1, replica_groups=mesh['mem'=2,'col'=16] {'mem'}, dimensions={1}, use_global_device_ids=true | all-gather | bytes 98304 | tf_op jit(solution)/shard_map/all_gather | solution.py:89
  6.7 4.6 %fusion.16 = bf16[512,16,32]{2,1,0:T(8,128)(2,1)S(1)} fusion(s32[512,16]{1,0:T(8,128)S(1)} %copy.40, bf16[32,65536]{1,0:T(8,128)(2,1)} %param.9), kind=kOutput, calls=%fused_computation.23 | convolution fusion | flops 68419584 | bytes 4751360 | tf_op jit(solution)/shard_map/kbc,bsc->kbs/dot_general | solution.py:64
  11.3 0.8 copy.43
  12.1 4.6 %fusion.13 = bf16[512,16,32]{2,1,0:T(8,128)(2,1)S(1)} fusion(s32[512,16]{1,0:T(8,128)S(1)} %copy.38, bf16[32,65536]{1,0:T(8,128)(2,1)} %param.8), kind=kOutput, calls=%fused_computation.22 | convolution fusion | flops 68419584 | bytes 4751360 | tf_op jit(solution)/shard_map/kbc,bsc->kbs/dot_general | solution.py:64
  16.7 0.8 copy.42
  17.5 1.1 pad_maximum_fusion
  18.6 3.6 %all-to-all-start = ((bf16[2,32,2,4096]{3,1,0,2:T(8,128)(2,1)}), bf16[2,32,2,4096]{3,1,0,2:T(8,128)(2,1)S(1)}, u32[]{:S(2)}, u32[]{:S(2)}) async-start(bf16[2,32,2,4096]{3,1,0,2:T(8,128)(2,1)} %pad_maximum_fusion), calls=%async_computation | async-start | bytes 2097152 | tf_op jit(solution)/shard_map/all_to_all | solution.py:93
  23.2 0.7 slice_reduce_fusion
  24.2 4.6 %copy.70 = bf16[4,2,8,32768]{3,2,0,1:T(8,128)(2,1)} copy(bf16[4,2,8,32768]{3,2,1,0:T(8,128)(2,1)} %bitcast.125) | data formatting | bytes 8388608 | tf_op jit(solution)/shard_map/reshape | solution.py:87
  28.8 2.3 %copy.71 = bf16[4,2,8,32768]{3,2,0,1:T(8,128)(2,1)} copy(bf16[4,2,8,32768]{3,2,1,0:T(8,128)(2,1)S(1)} %bitcast.126) | data formatting | bytes 8388608 | tf_op jit(solution)/shard_map/reshape | solution.py:87
  31.2 4.0 %all-to-all-done = bf16[2,32,2,4096]{3,1,0,2:T(8,128)(2,1)S(1)} async-done(((bf16[2,32,2,4096]{3,1,0,2:T(8,128)(2,1)}), bf16[2,32,2,4096]{3,1,0,2:T(8,128)(2,1)S(1)}, u32[]{:S(2)}, u32[]{:S(2)}) %all-to-all-start) | async-done | bytes 1048608 | tf_op jit(solution)/shard_map/all_to_all | solution.py:93
  35.1 5.6 %all-to-all-start.2 = ((bf16[32,2,32768]{2,0,1:T(8,128)(2,1)}), bf16[32,2,32768]{2,0,1:T(8,128)(2,1)}, u32[]{:S(2)}, u32[]{:S(2)}) async-start(bf16[32,2,32768]{2,0,1:T(8,128)(2,1)} %bitcast.124), calls=%async_computation.2 | async-start | bytes 8388608 | tf_op jit(solution)/shard_map/all_to_all | solution.py:104
  41.0 0.3 slice_reduce_fusion.2
  41.2 0.7 fusion.39
  41.9 0.6 fusion.38
  43.3 2.6 %maximum_add_fusion = f32[2]{0:T(128)S(1)} fusion(f32[1]{0:T(128)} %bitcast.10, f32[1]{0:T(128)} %bitcast.9, f32[1]{0:T(128)} %bitcast.14, f32[1]{0:T(128)} %bitcast.13), kind=kLoop, calls=%fused_computation.71 | loop fusion | flops 6 | bytes 24 | tf_op jit(solution)/shard_map/add | solution.py:100
  45.8 0.9 convolution_bitcast_fusion.1
  46.7 1.0 fusion.19
  47.7 1.0 fusion.25
  48.7 1.0 convolution_add_fusion.2
  49.8 39.4 %all-reduce.1 = (f32[64,64]{1,0:T(8,128)S(1)}, f32[2]{0:T(128)S(1)}, f32[64]{0:T(128)S(1)}) all-reduce(f32[64,64]{1,0:T(8,128)S(1)} %convolution_add_fusion.2, f32[2]{0:T(128)S(1)} %maximum_add_fusion, f32[64]{0:T(128)S(1)} %fusion.19), channel_id=1, replica_groups=mesh['mem'=2,'col'=16] {'mem'}, use_global_device_ids=true, to_apply=%region_8.0 | all-reduce | flops 4162 | bytes 33296 | tf_op jit(solution)/shard_map/psum | solution.py:10
  89.2 58.6 %all-reduce = (f32[64,64]{1,0:T(8,128)S(1)}, f32[2]{0:T(128)S(1)}, f32[64]{0:T(128)S(1)}) all-reduce(f32[64,64]{1,0:T(8,128)S(1)} %get-tuple-element.59, f32[2]{0:T(128)S(1)} %get-tuple-element.60, f32[64]{0:T(128)S(1)} %get-tuple-element.61), channel_id=1, replica_groups=mesh['mem'=2,'col'=16] {'col'}, use_global_device_ids=true, to_apply=%region_9.0 | all-reduce | flops 4162 | bytes 33296 | tf_op jit(solution)/shard_map/psum | solution.py:11
  147.8 0.6 fusion.53
  149.6 0.6 select_reduce_fusion
  150.9 0.6 multiply_reduce_fusion
  152.3 5.8 %all-to-all-start.1 = ((bf16[32,2,32768]{2,0,1:T(8,128)(2,1)}), bf16[32,2,32768]{2,0,1:T(8,128)(2,1)}, u32[]{:S(2)}, u32[]{:S(2)}) async-start(bf16[32,2,32768]{2,0,1:T(8,128)(2,1)} %bitcast.123), calls=%async_computation.1 | async-start | bytes 8388608 | tf_op jit(solution)/shard_map/all_to_all | solution.py:103
  158.1 15.5 %while.13 = (s32[]{:T(128)}, f32[64,64]{0,1:T(8,128)S(1)}, f32[64,64]{1,0:T(8,128)S(1)}, s32[]{:T(128)}) while((s32[]{:T(128)}, f32[64,64]{0,1:T(8,128)S(1)}, f32[64,64]{1,0:T(8,128)S(1)}, s32[]{:T(128)}) %tuple.41), condition=%wide.region_13.14_spmd.clone, body=%wide.region_12.13_spmd.clone.sunk | while | flops 9453570 | bytes 213045 | solution.py:26
  174.1 2.8 %fusion.42 = f32[1,32768]{1,0:T(1,128)S(1)} fusion(bf16[64,32768]{1,0:T(8,128)(2,1)} %bitcast.35), kind=kOutput, calls=%fused_computation.74 | convolution fusion | flops 4194304 | bytes 4325376 | tf_op jit(solution)/shard_map/dot_general | solution.py:115
  177.0 24.3 %all-to-all-done.1 = bf16[32,2,32768]{2,0,1:T(8,128)(2,1)} async-done(((bf16[32,2,32768]{2,0,1:T(8,128)(2,1)}), bf16[32,2,32768]{2,0,1:T(8,128)(2,1)}, u32[]{:S(2)}, u32[]{:S(2)}) %all-to-all-start.1) | async-done | bytes 4194336 | tf_op jit(solution)/shard_map/all_to_all | solution.py:103
  201.3 2.8 %fusion.44 = f32[1,32768]{1,0:T(1,128)S(1)} fusion(bf16[64,32768]{1,0:T(8,128)(2,1)} %bitcast.29), kind=kOutput, calls=%fused_computation.76 | convolution fusion | flops 4194304 | bytes 4325376 | tf_op jit(solution)/shard_map/dot_general | solution.py:115
  204.1 5.5 %fusion.4 = bf16[64,32768]{1,0:T(8,128)(2,1)} fusion(bf16[64,32768]{1,0:T(8,128)(2,1)} %bitcast.35, f32[32768]{0:T(1024)S(1)} %broadcast_multiply_fusion, f32[64]{0:T(128)S(1)} %broadcast_subtract_fusion, f32[64,64]{1,0:T(8,128)S(1)} %get-tuple-element.63), kind=kOutput, calls=%fused_computation.8 | convolution fusion | flops 274731008 | bytes 8536320 | tf_op jit(solution)/shard_map/dot_general | solution.py:116
  209.6 5.5 %fusion.3 = bf16[64,32768]{1,0:T(8,128)(2,1)} fusion(bf16[64,32768]{1,0:T(8,128)(2,1)} %bitcast.29, f32[64]{0:T(128)S(1)} %broadcast_subtract_fusion, f32[32768]{0:T(1024)S(1)} %broadcast_multiply_fusion.1, f32[64,64]{1,0:T(8,128)S(1)} %get-tuple-element.63), kind=kOutput, calls=%fused_computation.7 | convolution fusion | flops 274731008 | bytes 8536320 | tf_op jit(solution)/shard_map/dot_general | solution.py:116
  (165 shorter events, 17.2 us)
Async XLA Ops:
  16.6 5.5 %copy-start.3 = (f32[2,256,16]{1,2,0:T(8,128)S(1)}, f32[2,256,16]{1,2,0:T(8,128)}, u32[]{:S(2)}) copy-start(f32[2,256,16]{1,2,0:T(8,128)} %param.12) | copy-start | bytes 98308
  16.7 6.1 %copy-start.2 = (f32[2,256,16]{1,2,0:T(8,128)S(1)}, f32[2,256,16]{1,2,0:T(8,128)}, u32[]{:S(2)}) copy-start(f32[2,256,16]{1,2,0:T(8,128)} %param.13) | copy-start | bytes 98308
  16.7 6.4 %copy-start.4 = (s32[2,256]{1,0:T(2,128)S(1)}, s32[2,256]{1,0:T(2,128)}, u32[]{:S(2)}) copy-start(s32[2,256]{1,0:T(2,128)} %param.11) | copy-start | bytes 6148
  18.6 16.6 %all-to-all-start = ((bf16[2,32,2,4096]{3,1,0,2:T(8,128)(2,1)}), bf16[2,32,2,4096]{3,1,0,2:T(8,128)(2,1)S(1)}, u32[]{:S(2)}, u32[]{:S(2)}) async-start(bf16[2,32,2,4096]{3,1,0,2:T(8,128)(2,1)} %pad_maximum_fusion), calls=%async_computation | async-start | bytes 2097152 | tf_op jit(solution)/shard_map/all_to_all | solution.py:93
  24.1 4.6 %copy-start = (bf16[32,65536]{1,0:T(8,128)(2,1)S(1)}, bf16[32,65536]{1,0:T(8,128)(2,1)}, u32[]{:S(2)}) copy-start(bf16[32,65536]{1,0:T(8,128)(2,1)} %param.8) | copy-start | bytes 12582916
  35.1 117.2 %all-to-all-start.2 = ((bf16[32,2,32768]{2,0,1:T(8,128)(2,1)}), bf16[32,2,32768]{2,0,1:T(8,128)(2,1)}, u32[]{:S(2)}, u32[]{:S(2)}) async-start(bf16[32,2,32768]{2,0,1:T(8,128)(2,1)} %bitcast.124), calls=%async_computation.2 | async-start | bytes 8388608 | tf_op jit(solution)/shard_map/all_to_all | solution.py:104
  152.3 48.9 %all-to-all-start.1 = ((bf16[32,2,32768]{2,0,1:T(8,128)(2,1)}), bf16[32,2,32768]{2,0,1:T(8,128)(2,1)}, u32[]{:S(2)}, u32[]{:S(2)}) async-start(bf16[32,2,32768]{2,0,1:T(8,128)(2,1)} %bitcast.123), calls=%async_computation.1 | async-start | bytes 8388608 | tf_op jit(solution)/shard_map/all_to_all | solution.py:103
  174.1 35.5 %copy-start.1 = (f32[64,64]{1,0:T(8,128)}, f32[64,64]{1,0:T(8,128)S(1)}, u32[]{:S(2)}) copy-start(f32[64,64]{1,0:T(8,128)S(1)} %get-tuple-element.63) | copy-start | bytes 49156
